TPU v7x, 32 devices: a whole 2x2x4 slice. The times are simulated.
32 devices in a mesh: strip: 8 (over z, x), col: 4 (over y, core).
Axes of the slice: x: 2, y: 2, z: 4, core: 2. Of those that a mesh axis runs over, the one named last changes fastest.
Arguments:
- positions: float32 [3, 64, 1024], P(None, 'strip', 'col'), may hold values from -1.8 to 1.8
- target: float32 [3, 64, 1024], P(None, 'strip', 'col'), may hold values from -1.8 to 1.8
- inertia: float32 [64, 1024], P('strip', 'col'), may hold values from 1 to 4
- stiffness: float32 [3, 64, 1024], P(None, 'strip', 'col'), may hold values from 0.5 to 2
- pin_columns: int32 [64], replicated, may hold values from 0 to 1023
- inverses: bfloat16 [32, 512, 512], P('strip'), may hold values from -0.05 to 0.55
Outputs:
- displaced: float32 [3, 64, 1024], P(None, 'strip', 'col')
Inputs may be any that keep to these rules, and one draw needn't show every extreme that they name: `pin_columns`: a column may appear more than once.
All inputs are finite; a program needn't handle non-finite values.
Results may differ from a plain program's by a relative error of at most 0.0003.
Values sent between devices are 32-bit elements; how exact they have to be, the bound alone decides.
A program may use at most 128 MiB of HBM per device.

v0:
```python
import jax
import jax.numpy as jnp
from jax import lax
from jax.sharding import PartitionSpec as P

ITERS = 2


pin_stiffness = 20.0
highest = lax.Precision.HIGHEST


def passed_along(value, axis, steps):
    count = lax.axis_size(axis)
    initial, last = (max(0, -steps), min(count, count - steps))
    return lax.ppermute(value, axis, [(source, source + steps) for source in range(initial, last)])


def extended(cells, sides, width):
    for axis, dim in sides:
        count = lax.axis_size(axis)
        ends = count - 1
        head = lax.slice_in_dim(cells, 0, width, axis=dim)
        tail = lax.slice_in_dim(cells, cells.shape[dim] - width, cells.shape[dim], axis=dim)
        cells = jnp.concatenate(
            [
                lax.ppermute(tail, axis, [(i, (i + 1) % count) for i in range(ends)]),
                cells,
                lax.ppermute(head, axis, [((i + 1) % count, i) for i in range(ends)]),
            ],
            axis=dim,
        )
    return cells


def matmul(left_side, right_side):
    return jnp.dot(left_side, right_side, precision=highest, preferred_element_type=jnp.float32)


def times_transposed(rows_in, matrix):
    return lax.dot_general(
        rows_in,
        matrix,
        (((rows_in.ndim - 1,), (1,)), ((), ())),
        precision=highest,
        preferred_element_type=jnp.float32,
    )


def axis_vector(offset, direction):
    entries = [0.0, 0.0, 0.0]
    entries[direction] = float(offset)
    return jnp.array(entries, jnp.float32).reshape(3, 1, 1)


def edge_force(top_side, low_side, weight, rest_vec, rest_len):
    spacing = rest_vec + low_side - top_side
    length = jnp.sqrt(jnp.sum(spacing * spacing, axis=0, keepdims=True))
    projected = rest_len * spacing / jnp.maximum(length, 0.5 * rest_len)
    return weight[None] * (projected - rest_vec)


def spread(pulling, offset):
    return jnp.pad(-pulling, ((0, 0), (0, 0), (0, offset))) + jnp.pad(
        pulling, ((0, 0), (0, 0), (offset, 0))
    )


def shards(positions, target, inertia, stiffness, pin_columns, inverses):
    rows_dev = positions.shape[1]
    cols_dev = positions.shape[2]
    strips_dev = inverses.shape[0]
    strip_rows = rows_dev // strips_dev
    last_start = (strip_rows - 1) * cols_dev
    grid_rows = rows_dev * lax.axis_size("strip")
    grid_cols = cols_dev * lax.axis_size("col")
    row_start = lax.axis_index("strip") * rows_dev
    col_start = lax.axis_index("col") * cols_dev
    global_rows = row_start + jnp.arange(rows_dev, dtype=jnp.int32)
    wide_cols = col_start - 2 + jnp.arange(cols_dev + 4, dtype=jnp.int32)
    left_weights = passed_along(stiffness[:, :, -2:], "col", 1)
    right_blank = jnp.zeros((3, rows_dev, 2), jnp.float32)
    weights_ext = jnp.concatenate([left_weights, stiffness, right_blank], axis=2)
    edge_list = []
    for offset, channel in ((1, 0), (2, 2)):
        left_cols = wide_cols[: cols_dev + 4 - offset]
        inside = (left_cols >= 0) & (left_cols + offset <= grid_cols - 1)
        crossing = (left_cols + offset) // cols_dev != left_cols // cols_dev
        edge_weight = jnp.where(inside[None, :], weights_ext[channel][:, :-offset], 0.0)
        cross_weight = jnp.where(crossing[None, :], edge_weight, 0.0)
        edge_list.append((offset, edge_weight, cross_weight))
    vertical = jnp.where((global_rows < grid_rows - 1)[:, None], stiffness[1], 0.0)
    is_last = jnp.arange(rows_dev, dtype=jnp.int32) % strip_rows == strip_rows - 1
    weights_down = jnp.where(is_last[:, None], vertical, 0.0)
    weights_rows = vertical[strip_rows - 1 :: strip_rows][:, None, :]
    own_cols = col_start + jnp.arange(cols_dev, dtype=jnp.int32)
    pinned = jnp.any(pin_columns[:, None] == own_cols[None, :], axis=0) & (row_start == 0)
    pinned_row = jnp.where(pinned[None, :], positions[:, 0, :], 0.0)
    anchor = jnp.zeros_like(positions).at[:, 0, :].set(pinned_row)
    inertial = inertia[None] * target + pin_stiffness * anchor
    solve_mats = inverses.astype(jnp.float32)
    last_from_first = solve_mats[:, last_start:, :cols_dev]
    first_cols = solve_mats[:, :, :cols_dev]
    transfer = weights_rows.transpose(0, 2, 1) * last_from_first
    identity = jnp.eye(cols_dev, dtype=jnp.float32)

    def compose(product, factor):
        return (matmul(factor, product), None)

    device_map, unused = lax.scan(compose, identity, transfer)
    level_count = lax.axis_size("strip").bit_length() - 1
    distances = [1] + [2**step_index for step_index in range(level_count)]
    section_maps = []
    current = device_map
    for step_index in range(len(distances)):
        if step_index > 0:
            section_maps.append(current)
        if step_index < len(distances) - 1:
            received = passed_along(current, "strip", distances[step_index])
            current = received if step_index == 0 else matmul(current, received)

    def carry_offset(carried, inputs):
        last_rows, weight_row, matrix = inputs
        return (weight_row * (last_rows + times_transposed(carried, matrix)), None)

    def finish(carried, inputs):
        solved, weight_row, matrix = inputs
        complete = solved + times_transposed(carried, matrix)
        return (weight_row * complete[:, last_start:], complete)

    displaced = positions
    for sweep_number in range(ITERS):
        widened = extended(displaced, (("col", 2),), 2)
        summed = jnp.zeros_like(widened)
        coupled = jnp.zeros_like(widened)
        for offset, edge_weight, cross_weight in edge_list:
            pulling = edge_force(
                widened[:, :, :-offset],
                widened[:, :, offset:],
                edge_weight,
                axis_vector(offset, 0),
                float(offset),
            )
            summed = summed + spread(pulling, offset)
            coupled = coupled + jnp.pad(
                cross_weight[None] * widened[:, :, offset:], ((0, 0), (0, 0), (0, offset))
            )
            coupled = coupled + jnp.pad(
                cross_weight[None] * widened[:, :, :-offset], ((0, 0), (0, 0), (offset, 0))
            )
        forces = summed[:, :, 2:-2]
        coupling = coupled[:, :, 2:-2]
        internal = edge_force(
            displaced[:, :-1], displaced[:, 1:], vertical[:-1], axis_vector(1, 1), 1.0
        )
        forces = (
            forces
            + jnp.pad(-internal, ((0, 0), (0, 1), (0, 0)))
            + jnp.pad(internal, ((0, 0), (1, 0), (0, 0)))
        )
        next_row = passed_along(displaced[:, :1], "strip", -1)
        to_below = edge_force(displaced[:, -1:], next_row, vertical[-1:], axis_vector(1, 1), 1.0)
        from_above = passed_along(to_below, "strip", 1)
        forces = (
            forces
            + jnp.pad(-to_below, ((0, 0), (rows_dev - 1, 0), (0, 0)))
            + jnp.pad(from_above, ((0, 0), (0, rows_dev - 1), (0, 0)))
        )
        next_rows = jnp.concatenate([displaced[:, 1:], next_row], axis=1)
        rhs_field = inertial + forces + coupling + weights_down[None] * next_rows
        rhs_strips = rhs_field.reshape(3, strips_dev, strip_rows * cols_dev).transpose(1, 0, 2)
        base_solved = lax.dot_general(
            rhs_strips,
            solve_mats,
            (((2,), (2,)), ((0,), (0,))),
            precision=highest,
            preferred_element_type=jnp.float32,
        )
        zero_row = jnp.zeros((3, cols_dev), jnp.float32)
        device_offset, unused = lax.scan(
            carry_offset, zero_row, (base_solved[:, :, last_start:], weights_rows, last_from_first)
        )
        incoming = device_offset
        for step_index in range(len(distances)):
            received = passed_along(incoming, "strip", distances[step_index])
            incoming = (
                received
                if step_index == 0
                else times_transposed(received, section_maps[step_index - 1]) + incoming
            )
        unused, finished = lax.scan(finish, incoming, (base_solved, weights_rows, first_cols))
        displaced = finished.transpose(1, 0, 2).reshape(3, rows_dev, cols_dev)
    return displaced


def solution(mesh):
    in_specs = (
        P(None, "strip", "col"),
        P(None, "strip", "col"),
        P("strip", "col"),
        P(None, "strip", "col"),
        P(),
        P("strip", None, None),
    )
    out_specs = P(None, "strip", "col")
    return jax.shard_map(shards, mesh=mesh, in_specs=in_specs, out_specs=out_specs, check_vma=False)
```

profile of v0, /device:TPU:24, one launch (start us, length us, event | category | flops | bytes accessed | tf_op | source)
XLA Modules:
  0.0 141.2 jit_solution(14978460438340609339)
XLA Ops:
  1.4 2.3 %collective-permute-start = (f32[3,8,2]{2,1,0:T(8,128)}, f32[3,8,2]{2,1,0:T(8,128)}, u32[]{:S(2)}, u32[]{:S(2)}) collective-permute-start(f32[3,8,2]{2,1,0:T(8,128)} %slice.155), channel_id=1, source_target_pairs={{0,1},{1,2},{2,3},{4,5},{5,6},{6,7},{8,9},{9,10},{10,11},{12,13},{... | collective-permute-start | bytes 584 | tf_op jit(solution)/shard_map/ppermute | solution.py:16
  5.1 3.1 %collective-permute-start.1 = (f32[3,8,2]{2,1,0:T(8,128)}, f32[3,8,2]{2,1,0:T(8,128)S(1)}, u32[]{:S(2)}, u32[]{:S(2)}) collective-permute-start(f32[3,8,2]{2,1,0:T(8,128)} %get-tuple-element.292), channel_id=1, source_target_pairs={{0,1},{1,2},{2,3},{4,5},{5,6},{6,7},{8,9},{9,10},{10,11},{12,13},{... | collective-permute-start | bytes 584 | tf_op jit(solution)/shard_map/ppermute | solution.py:27
  11.6 3.3 %collective-permute-start.3 = (f32[3,1,256]{2,1,0:T(1,128)}, f32[3,1,256]{2,1,0:T(1,128)}, u32[]{:S(2)}, u32[]{:S(2)}) collective-permute-start(f32[3,1,256]{2,1,0:T(1,128)} %get-tuple-element.289), channel_id=1, source_target_pairs={{4,0},{8,4},{12,8},{16,12},{20,16},{24,20},{28,24},{5,1},{9,5},{13... | collective-permute-start | bytes 9224 | tf_op jit(solution)/shard_map/ppermute | solution.py:16
  15.8 2.2 %convert_element_type.38 = f32[4,512,512]{2,1,0:T(8,128)S(1)} convert(bf16[4,512,512]{2,1,0:T(8,128)(2,1)} %param.31) | non-fusion elementwise | flops 1048576 | bytes 6291456 | tf_op jit(solution)/shard_map/convert_element_type | solution.py:101
  18.2 1.7 %while.57 = (s32[]{:T(128)}, f32[256,256]{1,0:T(8,128)S(1)}, f32[4,256,256]{2,1,0:T(8,128)S(1)}, s32[]{:T(128)}) while((s32[]{:T(128)}, f32[256,256]{1,0:T(8,128)S(1)}, f32[4,256,256]{2,1,0:T(8,128)S(1)}, s32[]{:T(128)}) %tuple.121), condition=%wide.region_8.9_spmd, body=%wide.region_7.8_spmd.sunk | while | flops 201326592 | bytes 1310777 | solution.py:110
  19.9 3.3 %collective-permute-start.7 = (f32[256,256]{1,0:T(8,128)S(1)}, f32[256,256]{1,0:T(8,128)}, u32[]{:S(2)}, u32[]{:S(2)}) collective-permute-start(f32[256,256]{1,0:T(8,128)S(1)} %get-tuple-element.153), channel_id=1, source_target_pairs={{0,4},{4,8},{8,12},{12,16},{16,20},{20,24},{24,28},{1,5},{5,9},{9,... | collective-permute-start | bytes 786440 | tf_op jit(solution)/shard_map/ppermute | solution.py:16
  34.0 1.9 %collective-permute-start.4 = (f32[3,1,256]{2,1,0:T(1,128)S(1)}, f32[3,1,256]{2,1,0:T(1,128)S(1)}, u32[]{:S(2)}, u32[]{:S(2)}) collective-permute-start(f32[3,1,256]{2,1,0:T(1,128)S(1)} %get-tuple-element.256), channel_id=1, source_target_pairs={{0,4},{4,8},{8,12},{12,16},{16,20},{20,24},{24,28},{1,5},{5,9},{9,... | collective-permute-start | bytes 9224 | tf_op jit(solution)/shard_map/ppermute | solution.py:16
  36.7 3.7 %collective-permute-done.4 = f32[3,1,256]{2,1,0:T(1,128)S(1)} collective-permute-done((f32[3,1,256]{2,1,0:T(1,128)S(1)}, f32[3,1,256]{2,1,0:T(1,128)S(1)}, u32[]{:S(2)}, u32[]{:S(2)}) %collective-permute-start.4) | collective-permute-done | bytes 3104 | tf_op jit(solution)/shard_map/ppermute | solution.py:16
  41.2 1.7 %fusion.33 = f32[4,3,512]{2,1,0:T(4,128)S(1)} fusion(bf16[4,512,512]{2,1,0:T(8,128)(2,1)S(1)} %copy-done, f32[3,4,512]{2,1,0:T(4,128)S(1)} %reshape.181), kind=kOutput, calls=%fused_computation.75 | convolution fusion | flops 37748736 | bytes 2146304 | tf_op jit(solution)/shard_map/dot_general | solution.py:172
  43.0 1.9 %collective-permute-start.9 = (f32[256,256]{1,0:T(8,128)}, f32[256,256]{1,0:T(8,128)}, u32[]{:S(2)}, u32[]{:S(2)}) collective-permute-start(f32[256,256]{1,0:T(8,128)} %collective-permute-done.7), channel_id=1, source_target_pairs={{0,4},{4,8},{8,12},{12,16},{16,20},{20,24},{24,28},{1,5},{5,9},{9,... | collective-permute-start | bytes 786440 | tf_op jit(solution)/shard_map/ppermute | solution.py:16
  46.3 2.0 %collective-permute-start.5 = (f32[3,256]{1,0:T(4,128)S(1)}, f32[3,256]{1,0:T(4,128)S(1)}, u32[]{:S(2)}, u32[]{:S(2)}) collective-permute-start(f32[3,256]{1,0:T(4,128)S(1)} %get-tuple-element.152), channel_id=1, source_target_pairs={{0,4},{4,8},{8,12},{12,16},{16,20},{20,24},{24,28},{1,5},{5,9},{9,... | collective-permute-start | bytes 9224 | tf_op jit(solution)/shard_map/ppermute | solution.py:16
  48.3 5.5 %collective-permute-done.5 = f32[3,256]{1,0:T(4,128)S(1)} collective-permute-done((f32[3,256]{1,0:T(4,128)S(1)}, f32[3,256]{1,0:T(4,128)S(1)}, u32[]{:S(2)}, u32[]{:S(2)}) %collective-permute-start.5) | collective-permute-done | bytes 3104 | tf_op jit(solution)/shard_map/ppermute | solution.py:16
  53.8 1.9 %collective-permute-start.6 = (f32[3,256]{1,0:T(4,128)S(1)}, f32[3,256]{1,0:T(4,128)S(1)}, u32[]{:S(2)}, u32[]{:S(2)}) collective-permute-start(f32[3,256]{1,0:T(4,128)S(1)} %collective-permute-done.5), channel_id=1, source_target_pairs={{0,4},{4,8},{8,12},{12,16},{16,20},{20,24},{24,28},{1,5},{5,9},{9,... | collective-permute-start | bytes 9224 | tf_op jit(solution)/shard_map/ppermute | solution.py:16
  58.4 1.7 %collective-permute-done.6 = f32[3,256]{1,0:T(4,128)S(1)} collective-permute-done((f32[3,256]{1,0:T(4,128)S(1)}, f32[3,256]{1,0:T(4,128)S(1)}, u32[]{:S(2)}, u32[]{:S(2)}) %collective-permute-start.6) | collective-permute-done | bytes 3104 | tf_op jit(solution)/shard_map/ppermute | solution.py:16
  64.2 2.7 %collective-permute-done.8 = f32[3,256]{1,0:T(4,128)S(1)} collective-permute-done((f32[3,256]{1,0:T(4,128)S(1)}, f32[3,256]{1,0:T(4,128)S(1)}, u32[]{:S(2)}, u32[]{:S(2)}) %collective-permute-start.8) | collective-permute-done | bytes 3104 | tf_op jit(solution)/shard_map/ppermute | solution.py:16
  69.9 3.7 %collective-permute-done.10 = f32[3,256]{1,0:T(4,128)S(1)} collective-permute-done((f32[3,256]{1,0:T(4,128)S(1)}, f32[3,256]{1,0:T(4,128)S(1)}, u32[]{:S(2)}, u32[]{:S(2)}) %collective-permute-start.10) | collective-permute-done | bytes 3104 | tf_op jit(solution)/shard_map/ppermute | solution.py:16
  74.0 6.6 %while.58 = (s32[]{:T(128)}, f32[3,256]{1,0:T(4,128)S(1)}, f32[4,3,512]{2,1,0:T(4,128)S(1)}, f32[4,1,256]{2,1,0:T(1,128)S(1)}, f32[4,3,512]{2,1,0:T(4,128)S(1)}, /*index=5*/f32[4,512,256]{2,1,0:T(8,128)}, s32[]{:T(128)}) while((s32[]{:T(128)}, f32[3,256]{1,0:T(4,128)S(1)}, f32[4,3,512]{2,1,0:T(4,128)S(1)}, f32[4,1,256]{2,1,0:T(1,128)S(1)}, ...), condition=%wide.region_10.11_spmd, body=%wide.region_9.10_spmd.sunk | while | flops 4720898 | bytes 563281 | solution.py:191
  74.0 1.6 %bitcast_dynamic-update-slice_fusion.4 = (f32[4,3,512]{2,1,0:T(4,128)S(1)}, f32[3,512]{1,0:T(4,128)S(1)}) fusion(f32[4,3,512]{2,1,0:T(4,128)S(1)} %get-tuple-element.502, s32[]{:T(128)} %get-tuple-element.500, f32[3,256]{1,0:T(4,128)S(1)} %get-tuple-element.501, f32[4,512,256]{2,1,0:T(8,128)} %get-tuple-element.512, ...), kind=kOutput, calls=%fused_computation.8.clone.1 | convolution fusion | flops 4720128 | bytes 553984 | tf_op jit(solution)/shard_map/while/body/eval_jaxpr/dot_general | solution.py:41
  77.3 1.6 %bitcast_dynamic-update-slice_fusion.4 = (f32[4,3,512]{2,1,0:T(4,128)S(1)}, f32[3,512]{1,0:T(4,128)S(1)}) fusion(f32[4,3,512]{2,1,0:T(4,128)S(1)} %get-tuple-element.502, s32[]{:T(128)} %get-tuple-element.500, f32[3,256]{1,0:T(4,128)S(1)} %get-tuple-element.501, f32[4,512,256]{2,1,0:T(8,128)} %get-tuple-element.512, ...), kind=kOutput, calls=%fused_computation.8.clone.1 | convolution fusion | flops 4720128 | bytes 553984 | tf_op jit(solution)/shard_map/while/body/eval_jaxpr/dot_general | solution.py:41
  82.7 3.7 %collective-permute-start.14 = (f32[3,1,256]{2,1,0:T(1,128)S(1)}, f32[3,1,256]{2,1,0:T(1,128)S(1)}, u32[]{:S(2)}, u32[]{:S(2)}) collective-permute-start(f32[3,1,256]{2,1,0:T(1,128)S(1)} %slice.205), channel_id=1, source_target_pairs={{4,0},{8,4},{12,8},{16,12},{20,16},{24,20},{28,24},{5,1},{9,5},{13... | collective-permute-start | bytes 9224 | tf_op jit(solution)/shard_map/ppermute | solution.py:16
  89.8 3.2 %collective-permute-done.13 = f32[3,8,2]{2,1,0:T(8,128)S(1)} collective-permute-done((f32[3,8,2]{2,1,0:T(8,128)S(1)}, f32[3,8,2]{2,1,0:T(8,128)S(1)}, u32[]{:S(2)}, u32[]{:S(2)}) %collective-permute-start.13) | collective-permute-done | bytes 224 | tf_op jit(solution)/shard_map/ppermute | solution.py:29
  97.0 2.2 %collective-permute-start.15 = (f32[3,1,256]{2,1,0:T(1,128)S(1)}, f32[3,1,256]{2,1,0:T(1,128)S(1)}, u32[]{:S(2)}, u32[]{:S(2)}) collective-permute-start(f32[3,1,256]{2,1,0:T(1,128)S(1)} %get-tuple-element.246), channel_id=1, source_target_pairs={{0,4},{4,8},{8,12},{12,16},{16,20},{20,24},{24,28},{1,5},{5,9},{9,... | collective-permute-start | bytes 9224 | tf_op jit(solution)/shard_map/ppermute | solution.py:16
  99.9 3.4 %collective-permute-done.15 = f32[3,1,256]{2,1,0:T(1,128)S(1)} collective-permute-done((f32[3,1,256]{2,1,0:T(1,128)S(1)}, f32[3,1,256]{2,1,0:T(1,128)S(1)}, u32[]{:S(2)}, u32[]{:S(2)}) %collective-permute-start.15) | collective-permute-done | bytes 3104 | tf_op jit(solution)/shard_map/ppermute | solution.py:16
  104.3 1.7 %fusion.31 = f32[4,3,512]{2,1,0:T(4,128)S(1)} fusion(bf16[4,512,512]{2,1,0:T(8,128)(2,1)S(1)} %copy-done, f32[3,4,512]{2,1,0:T(4,128)S(1)} %reshape.183), kind=kOutput, calls=%fused_computation.73 | convolution fusion | flops 37748736 | bytes 2146304 | tf_op jit(solution)/shard_map/dot_general | solution.py:172
  107.4 2.0 %collective-permute-start.16 = (f32[3,256]{1,0:T(4,128)S(1)}, f32[3,256]{1,0:T(4,128)S(1)}, u32[]{:S(2)}, u32[]{:S(2)}) collective-permute-start(f32[3,256]{1,0:T(4,128)S(1)} %get-tuple-element.155), channel_id=1, source_target_pairs={{0,4},{4,8},{8,12},{12,16},{16,20},{20,24},{24,28},{1,5},{5,9},{9,... | collective-permute-start | bytes 9224 | tf_op jit(solution)/shard_map/ppermute | solution.py:16
  109.3 4.5 %collective-permute-done.16 = f32[3,256]{1,0:T(4,128)S(1)} collective-permute-done((f32[3,256]{1,0:T(4,128)S(1)}, f32[3,256]{1,0:T(4,128)S(1)}, u32[]{:S(2)}, u32[]{:S(2)}) %collective-permute-start.16) | collective-permute-done | bytes 3104 | tf_op jit(solution)/shard_map/ppermute | solution.py:16
  113.8 1.9 %collective-permute-start.17 = (f32[3,256]{1,0:T(4,128)S(1)}, f32[3,256]{1,0:T(4,128)S(1)}, u32[]{:S(2)}, u32[]{:S(2)}) collective-permute-start(f32[3,256]{1,0:T(4,128)S(1)} %collective-permute-done.16), channel_id=1, source_target_pairs={{0,4},{4,8},{8,12},{12,16},{16,20},{20,24},{24,28},{1,5},{5,9},{9,... | collective-permute-start | bytes 9224 | tf_op jit(solution)/shard_map/ppermute | solution.py:16
  115.7 4.5 %collective-permute-done.17 = f32[3,256]{1,0:T(4,128)S(1)} collective-permute-done((f32[3,256]{1,0:T(4,128)S(1)}, f32[3,256]{1,0:T(4,128)S(1)}, u32[]{:S(2)}, u32[]{:S(2)}) %collective-permute-start.17) | collective-permute-done | bytes 3104 | tf_op jit(solution)/shard_map/ppermute | solution.py:16
  122.8 4.2 %collective-permute-done.18 = f32[3,256]{1,0:T(4,128)S(1)} collective-permute-done((f32[3,256]{1,0:T(4,128)S(1)}, f32[3,256]{1,0:T(4,128)S(1)}, u32[]{:S(2)}, u32[]{:S(2)}) %collective-permute-start.18) | collective-permute-done | bytes 3104 | tf_op jit(solution)/shard_map/ppermute | solution.py:16
  128.6 5.1 %collective-permute-done.19 = f32[3,256]{1,0:T(4,128)S(1)} collective-permute-done((f32[3,256]{1,0:T(4,128)S(1)}, f32[3,256]{1,0:T(4,128)S(1)}, u32[]{:S(2)}, u32[]{:S(2)}) %collective-permute-start.19) | collective-permute-done | bytes 3104 | tf_op jit(solution)/shard_map/ppermute | solution.py:16
  134.0 6.6 %while.59 = (s32[]{:T(128)}, f32[3,256]{1,0:T(4,128)S(1)}, f32[4,3,512]{2,1,0:T(4,128)S(1)}, f32[4,1,256]{2,1,0:T(1,128)S(1)}, f32[4,3,512]{2,1,0:T(4,128)S(1)}, /*index=5*/f32[4,512,256]{2,1,0:T(8,128)}, s32[]{:T(128)}) while((s32[]{:T(128)}, f32[3,256]{1,0:T(4,128)S(1)}, f32[4,3,512]{2,1,0:T(4,128)S(1)}, f32[4,1,256]{2,1,0:T(1,128)S(1)}, ...), condition=%wide.region_18.19_spmd, body=%wide.region_17.18_spmd.sunk | while | flops 4720898 | bytes 563281 | solution.py:191
  135.7 1.6 %bitcast_dynamic-update-slice_fusion.5 = (f32[4,3,512]{2,1,0:T(4,128)S(1)}, f32[3,512]{1,0:T(4,128)S(1)}) fusion(f32[4,3,512]{2,1,0:T(4,128)S(1)} %get-tuple-element.544, s32[]{:T(128)} %get-tuple-element.542, f32[3,256]{1,0:T(4,128)S(1)} %get-tuple-element.543, f32[4,512,256]{2,1,0:T(8,128)} %get-tuple-element.554, ...), kind=kOutput, calls=%fused_computation.16.clone.1 | convolution fusion | flops 4720128 | bytes 553984 | tf_op jit(solution)/shard_map/while/body/eval_jaxpr/dot_general | solution.py:41
  (174 shorter events, 60.4 us)
Async XLA Ops:
  1.4 25.8 %collective-permute-start = (f32[3,8,2]{2,1,0:T(8,128)}, f32[3,8,2]{2,1,0:T(8,128)}, u32[]{:S(2)}, u32[]{:S(2)}) collective-permute-start(f32[3,8,2]{2,1,0:T(8,128)} %slice.155), channel_id=1, source_target_pairs={{0,1},{1,2},{2,3},{4,5},{5,6},{6,7},{8,9},{9,10},{10,11},{12,13},{... | collective-permute-start | bytes 584 | tf_op jit(solution)/shard_map/ppermute | solution.py:16
  5.1 22.9 %collective-permute-start.1 = (f32[3,8,2]{2,1,0:T(8,128)}, f32[3,8,2]{2,1,0:T(8,128)S(1)}, u32[]{:S(2)}, u32[]{:S(2)}) collective-permute-start(f32[3,8,2]{2,1,0:T(8,128)} %get-tuple-element.292), channel_id=1, source_target_pairs={{0,1},{1,2},{2,3},{4,5},{5,6},{6,7},{8,9},{9,10},{10,11},{12,13},{... | collective-permute-start | bytes 584 | tf_op jit(solution)/shard_map/ppermute | solution.py:27
  8.2 19.8 %collective-permute-start.2 = (f32[3,8,2]{2,1,0:T(8,128)}, f32[3,8,2]{2,1,0:T(8,128)S(1)}, u32[]{:S(2)}, u32[]{:S(2)}) collective-permute-start(f32[3,8,2]{2,1,0:T(8,128)} %get-tuple-element.291), channel_id=1, source_target_pairs={{1,0},{2,1},{3,2},{5,4},{6,5},{7,6},{9,8},{10,9},{11,10},{13,12},{... | collective-permute-start | bytes 584 | tf_op jit(solution)/shard_map/ppermute | solution.py:29
  11.6 20.8 %collective-permute-start.3 = (f32[3,1,256]{2,1,0:T(1,128)}, f32[3,1,256]{2,1,0:T(1,128)}, u32[]{:S(2)}, u32[]{:S(2)}) collective-permute-start(f32[3,1,256]{2,1,0:T(1,128)} %get-tuple-element.289), channel_id=1, source_target_pairs={{4,0},{8,4},{12,8},{16,12},{20,16},{24,20},{28,24},{5,1},{9,5},{13... | collective-permute-start | bytes 9224 | tf_op jit(solution)/shard_map/ppermute | solution.py:16
  14.9 3.0 %copy-start.10 = (pred[8]{0:T(512)(128)(4,1)}, pred[8]{0:T(512)(128)(4,1)S(1)}, u32[]{:S(2)}) copy-start(pred[8]{0:T(512)(128)(4,1)S(1)} %add_compare_fusion) | copy-start | bytes 28
  17.9 7.5 %copy-start = (bf16[4,512,512]{2,1,0:T(8,128)(2,1)S(1)}, bf16[4,512,512]{2,1,0:T(8,128)(2,1)}, u32[]{:S(2)}) copy-start(bf16[4,512,512]{2,1,0:T(8,128)(2,1)} %param.31) | copy-start | bytes 6291460
  18.2 6.2 %copy-start.3 = (f32[3,8,256]{2,1,0:T(8,128)S(1)}, f32[3,8,256]{2,1,0:T(8,128)}, u32[]{:S(2)}) copy-start(f32[3,8,256]{2,1,0:T(8,128)} %param.26) | copy-start | bytes 73732
  19.9 5.6 %copy-start.9 = (f32[3]{0:T(128)S(1)}, f32[3]{0:T(128)}, u32[]{:S(2)}) copy-start(f32[3]{0:T(128)} %constant.175.clone) | copy-start | bytes 40
  19.9 5.7 %copy-start.4 = (f32[3,8,256]{2,1,0:T(8,128)S(1)}, f32[3,8,256]{2,1,0:T(8,128)}, u32[]{:S(2)}) copy-start(f32[3,8,256]{2,1,0:T(8,128)} %param.29) | copy-start | bytes 73732
  19.9 20.4 %copy-start.7 = (f32[8,256]{1,0:T(8,128)S(1)}, f32[8,256]{1,0:T(8,128)}, u32[]{:S(2)}) copy-start(f32[8,256]{1,0:T(8,128)} %param.28) | copy-start | bytes 24580
  19.9 23.0 %collective-permute-start.7 = (f32[256,256]{1,0:T(8,128)S(1)}, f32[256,256]{1,0:T(8,128)}, u32[]{:S(2)}, u32[]{:S(2)}) collective-permute-start(f32[256,256]{1,0:T(8,128)S(1)} %get-tuple-element.153), channel_id=1, source_target_pairs={{0,4},{4,8},{8,12},{12,16},{16,20},{20,24},{24,28},{1,5},{5,9},{9,... | collective-permute-start | bytes 786440 | tf_op jit(solution)/shard_map/ppermute | solution.py:16
  26.4 14.0 %copy-start.5 = (f32[8,256]{1,0:T(8,128)}, f32[8,256]{1,0:T(8,128)S(1)}, u32[]{:S(2)}) copy-start(f32[8,256]{1,0:T(8,128)S(1)} %select_bitcast_fusion) | copy-start | bytes 24580
  28.0 0.9 copy-start.6
  34.0 6.4 %collective-permute-start.4 = (f32[3,1,256]{2,1,0:T(1,128)S(1)}, f32[3,1,256]{2,1,0:T(1,128)S(1)}, u32[]{:S(2)}, u32[]{:S(2)}) collective-permute-start(f32[3,1,256]{2,1,0:T(1,128)S(1)} %get-tuple-element.256), channel_id=1, source_target_pairs={{0,4},{4,8},{8,12},{12,16},{16,20},{20,24},{24,28},{1,5},{5,9},{9,... | collective-permute-start | bytes 9224 | tf_op jit(solution)/shard_map/ppermute | solution.py:16
  43.0 12.7 %collective-permute-start.9 = (f32[256,256]{1,0:T(8,128)}, f32[256,256]{1,0:T(8,128)}, u32[]{:S(2)}, u32[]{:S(2)}) collective-permute-start(f32[256,256]{1,0:T(8,128)} %collective-permute-done.7), channel_id=1, source_target_pairs={{0,4},{4,8},{8,12},{12,16},{16,20},{20,24},{24,28},{1,5},{5,9},{9,... | collective-permute-start | bytes 786440 | tf_op jit(solution)/shard_map/ppermute | solution.py:16
  46.3 7.5 %collective-permute-start.5 = (f32[3,256]{1,0:T(4,128)S(1)}, f32[3,256]{1,0:T(4,128)S(1)}, u32[]{:S(2)}, u32[]{:S(2)}) collective-permute-start(f32[3,256]{1,0:T(4,128)S(1)} %get-tuple-element.152), channel_id=1, source_target_pairs={{0,4},{4,8},{8,12},{12,16},{16,20},{20,24},{24,28},{1,5},{5,9},{9,... | collective-permute-start | bytes 9224 | tf_op jit(solution)/shard_map/ppermute | solution.py:16
  53.8 6.4 %collective-permute-start.6 = (f32[3,256]{1,0:T(4,128)S(1)}, f32[3,256]{1,0:T(4,128)S(1)}, u32[]{:S(2)}, u32[]{:S(2)}) collective-permute-start(f32[3,256]{1,0:T(4,128)S(1)} %collective-permute-done.5), channel_id=1, source_target_pairs={{0,4},{4,8},{8,12},{12,16},{16,20},{20,24},{24,28},{1,5},{5,9},{9,... | collective-permute-start | bytes 9224 | tf_op jit(solution)/shard_map/ppermute | solution.py:16
  57.1 11.4 %collective-permute-start.11 = (f32[256,256]{1,0:T(8,128)S(1)}, f32[256,256]{1,0:T(8,128)}, u32[]{:S(2)}, u32[]{:S(2)}) collective-permute-start(f32[256,256]{1,0:T(8,128)S(1)} %fusion.76), channel_id=1, source_target_pairs={{0,8},{4,12},{8,16},{12,20},{16,24},{20,28},{1,9},{5,13},{9,17},{1... | collective-permute-start | bytes 786440 | tf_op jit(solution)/shard_map/ppermute | solution.py:16
  61.4 5.6 %collective-permute-start.8 = (f32[3,256]{1,0:T(4,128)S(1)}, f32[3,256]{1,0:T(4,128)S(1)}, u32[]{:S(2)}, u32[]{:S(2)}) collective-permute-start(f32[3,256]{1,0:T(4,128)S(1)} %convolution_add_fusion.5), channel_id=1, source_target_pairs={{0,8},{4,12},{8,16},{12,20},{16,24},{20,28},{1,9},{5,13},{9,17},{1... | collective-permute-start | bytes 9224 | tf_op jit(solution)/shard_map/ppermute | solution.py:16
  67.2 6.5 %collective-permute-start.10 = (f32[3,256]{1,0:T(4,128)S(1)}, f32[3,256]{1,0:T(4,128)S(1)}, u32[]{:S(2)}, u32[]{:S(2)}) collective-permute-start(f32[3,256]{1,0:T(4,128)S(1)} %convolution_add_fusion.4), channel_id=1, source_target_pairs={{0,16},{4,20},{8,24},{12,28},{1,17},{5,21},{9,25},{13,29},{2,18},{... | collective-permute-start | bytes 9224 | tf_op jit(solution)/shard_map/ppermute | solution.py:16
  69.9 3.8 %copy-start.1 = (f32[256,256]{1,0:T(8,128)}, f32[256,256]{1,0:T(8,128)S(1)}, u32[]{:S(2)}) copy-start(f32[256,256]{1,0:T(8,128)S(1)} %fusion.77) | copy-start | bytes 786436
  74.0 29.4 %copy-start.8 = (f32[3,1,256]{2,1,0:T(1,128)S(1)}, f32[3,1,256]{2,1,0:T(1,128)}, u32[]{:S(2)}) copy-start(f32[3,1,256]{2,1,0:T(1,128)} %get-tuple-element.288) | copy-start | bytes 9220
  82.7 12.7 %collective-permute-start.14 = (f32[3,1,256]{2,1,0:T(1,128)S(1)}, f32[3,1,256]{2,1,0:T(1,128)S(1)}, u32[]{:S(2)}, u32[]{:S(2)}) collective-permute-start(f32[3,1,256]{2,1,0:T(1,128)S(1)} %slice.205), channel_id=1, source_target_pairs={{4,0},{8,4},{12,8},{16,12},{20,16},{24,20},{28,24},{5,1},{9,5},{13... | collective-permute-start | bytes 9224 | tf_op jit(solution)/shard_map/ppermute | solution.py:16
  87.2 2.6 %collective-permute-start.12 = (f32[3,8,2]{2,1,0:T(8,128)S(1)}, f32[3,8,2]{2,1,0:T(8,128)S(1)}, u32[]{:S(2)}, u32[]{:S(2)}) collective-permute-start(f32[3,8,2]{2,1,0:T(8,128)S(1)} %get-tuple-element.287), channel_id=1, source_target_pairs={{0,1},{1,2},{2,3},{4,5},{5,6},{6,7},{8,9},{9,10},{10,11},{12,13},{... | collective-permute-start | bytes 584 | tf_op jit(solution)/shard_map/ppermute | solution.py:27
  88.5 4.5 %collective-permute-start.13 = (f32[3,8,2]{2,1,0:T(8,128)S(1)}, f32[3,8,2]{2,1,0:T(8,128)S(1)}, u32[]{:S(2)}, u32[]{:S(2)}) collective-permute-start(f32[3,8,2]{2,1,0:T(8,128)S(1)} %get-tuple-element.286), channel_id=1, source_target_pairs={{1,0},{2,1},{3,2},{5,4},{6,5},{7,6},{9,8},{10,9},{11,10},{13,12},{... | collective-permute-start | bytes 584 | tf_op jit(solution)/shard_map/ppermute | solution.py:29
  97.0 6.4 %collective-permute-start.15 = (f32[3,1,256]{2,1,0:T(1,128)S(1)}, f32[3,1,256]{2,1,0:T(1,128)S(1)}, u32[]{:S(2)}, u32[]{:S(2)}) collective-permute-start(f32[3,1,256]{2,1,0:T(1,128)S(1)} %get-tuple-element.246), channel_id=1, source_target_pairs={{0,4},{4,8},{8,12},{12,16},{16,20},{20,24},{24,28},{1,5},{5,9},{9,... | collective-permute-start | bytes 9224 | tf_op jit(solution)/shard_map/ppermute | solution.py:16
  106.0 27.7 %copy-start.2 = (f32[256,256]{1,0:T(8,128)S(1)}, f32[256,256]{1,0:T(8,128)}, u32[]{:S(2)}) copy-start(f32[256,256]{1,0:T(8,128)} %copy-done.1) | copy-start | bytes 786436
  107.4 6.4 %collective-permute-start.16 = (f32[3,256]{1,0:T(4,128)S(1)}, f32[3,256]{1,0:T(4,128)S(1)}, u32[]{:S(2)}, u32[]{:S(2)}) collective-permute-start(f32[3,256]{1,0:T(4,128)S(1)} %get-tuple-element.155), channel_id=1, source_target_pairs={{0,4},{4,8},{8,12},{12,16},{16,20},{20,24},{24,28},{1,5},{5,9},{9,... | collective-permute-start | bytes 9224 | tf_op jit(solution)/shard_map/ppermute | solution.py:16
  113.8 6.4 %collective-permute-start.17 = (f32[3,256]{1,0:T(4,128)S(1)}, f32[3,256]{1,0:T(4,128)S(1)}, u32[]{:S(2)}, u32[]{:S(2)}) collective-permute-start(f32[3,256]{1,0:T(4,128)S(1)} %collective-permute-done.16), channel_id=1, source_target_pairs={{0,4},{4,8},{8,12},{12,16},{16,20},{20,24},{24,28},{1,5},{5,9},{9,... | collective-permute-start | bytes 9224 | tf_op jit(solution)/shard_map/ppermute | solution.py:16
  121.4 5.6 %collective-permute-start.18 = (f32[3,256]{1,0:T(4,128)S(1)}, f32[3,256]{1,0:T(4,128)S(1)}, u32[]{:S(2)}, u32[]{:S(2)}) collective-permute-start(f32[3,256]{1,0:T(4,128)S(1)} %convolution_add_fusion.2), channel_id=1, source_target_pairs={{0,8},{4,12},{8,16},{12,20},{16,24},{20,28},{1,9},{5,13},{9,17},{1... | collective-permute-start | bytes 9224 | tf_op jit(solution)/shard_map/ppermute | solution.py:16
  127.2 6.5 %collective-permute-start.19 = (f32[3,256]{1,0:T(4,128)S(1)}, f32[3,256]{1,0:T(4,128)S(1)}, u32[]{:S(2)}, u32[]{:S(2)}) collective-permute-start(f32[3,256]{1,0:T(4,128)S(1)} %convolution_add_fusion.1), channel_id=1, source_target_pairs={{0,16},{4,20},{8,24},{12,28},{1,17},{5,21},{9,25},{13,29},{2,18},{... | collective-permute-start | bytes 9224 | tf_op jit(solution)/shard_map/ppermute | solution.py:16
where the time goes:
time: 144 us; the launch traced here: 141 us
  waiting for transfers between devices  42.3 us (29%)
  starting transfers between devices  39.9 us (28%)
  matrix products  26.2 us (18%)
  other arithmetic  23 us (16%)
  local copies, waits for them, and re-layouts  8.26 us (6%)
    ppermute x16, waiting for transfers between devices, passed_along(): lax.ppermute(value, axis, [(source, source + steps) for source in range(i...  39.1 us
    ppermute x16, starting transfers between devices, passed_along(): lax.ppermute(value, axis, [(source, source + steps) for source in range(i...  33 us
    dot_general x22, matrix products, times_transposed(): lax.dot_general(rows_in, matrix, (((rows_in.ndim - 1,), (1,)), ((), ())),...  18.5 us
    reduce_sum x8, other arithmetic, edge_force(): length = jnp.sqrt(jnp.sum(spacing * spacing, axis=0, keepdims=True))  5.31 us
    ppermute x2, starting transfers between devices, extended(): lax.ppermute(tail, axis, [(i, (i + 1) % count) for i in range(ends)])  4.4 us
    dot_general x6, matrix products, matmul(): jnp.dot(left_side, right_side, precision=highest, preferred_element_type=...  4.27 us
    dot_general x2, matrix products, shards(): lax.dot_general(rhs_strips, solve_mats, (((2,), (2,)), ((0,), (0,))), pre...  3.44 us
    ppermute x2, waiting for transfers between devices, extended(): lax.ppermute(head, axis, [((i + 1) % count, i) for i in range(ends)])  3.21 us
  transfers between devices with their start and end apart: 20, of which 11 were waited for; matrix products, arithmetic and copies ran while one was open for 23% of the time, Pallas kernels for 0%

commit v1 on v0

v1 whole, which is shorter than its diff:
```python
import functools

import jax
import jax.numpy as jnp
from jax import lax
from jax.experimental import pallas as pl
from jax.experimental.pallas import tpu as pltpu
from jax.sharding import PartitionSpec as P

ITERS = 2

pin_stiffness = 20.0
SUB = 8
LANES = 128
MESH = pl.DeviceIdType.MESH
f32 = jnp.float32
bf16 = jnp.bfloat16

TO_RIGHT, TO_LEFT, UP, DOWN = range(4)


def split(v):
    high = v.astype(bf16).astype(f32)
    return jnp.concatenate([high, v - high], axis=0).astype(bf16)


def folded(product):
    half = product.shape[0] // 2
    return product[:half] + product[half:]


def times_transposed(parts, matrix):
    product = lax.dot_general(
        parts, matrix, (((1,), (1,)), ((), ())), preferred_element_type=f32
    )
    return folded(product)


def times_pair(parts, high, low):
    product = jnp.dot(parts, high, preferred_element_type=f32) + jnp.dot(
        parts, low, preferred_element_type=f32
    )
    return folded(product)


def stretch(squared, rest_len):
    return rest_len * jnp.minimum(lax.rsqrt(squared), 2.0 / rest_len)


def kernel(
    n_strip, n_col,
    pins, pos, tgt, inertia, stf, inv,
    out,
    mats, high, low, disp, halo, halo_w, send_row, recv_row, edge_w, cross_w,
    inv_sem, side_send, side_recv, w_send, w_recv, row_send, row_recv,
):
    rows, cols = pos.shape[1], pos.shape[2]
    strips = inv.shape[0]
    srows = rows // strips
    block = srows * cols
    last_start = block - cols
    me_s, me_c = lax.axis_index("strip"), lax.axis_index("col")
    not_top, not_bottom = me_s > 0, me_s < n_strip - 1
    not_left, not_right = me_c > 0, me_c < n_col - 1

    loads = [pltpu.make_async_copy(inv.at[k], mats.at[k], inv_sem.at[k]) for k in range(strips)]
    for load in loads:
        load.start()

    barrier = pltpu.get_barrier_semaphore()
    sides = (
        (not_top, (me_s - 1, me_c)),
        (not_bottom, (me_s + 1, me_c)),
        (not_left, (me_s, me_c - 1)),
        (not_right, (me_s, me_c + 1)),
    )
    for there, device in sides:
        @pl.when(there)
        def _():
            pl.semaphore_signal(barrier, inc=1, device_id=device, device_id_type=MESH)

    def side_copies(sweep):
        source = pos if sweep == 0 else disp
        right = pltpu.make_async_remote_copy(
            src_ref=source.at[:, :, pl.ds(cols - LANES, LANES)], dst_ref=halo.at[sweep, 0],
            send_sem=side_send.at[sweep, 0], recv_sem=side_recv.at[sweep, 0],
            device_id=(me_s, me_c + 1), device_id_type=MESH)
        left = pltpu.make_async_remote_copy(
            src_ref=source.at[:, :, pl.ds(0, LANES)], dst_ref=halo.at[sweep, 1],
            send_sem=side_send.at[sweep, 1], recv_sem=side_recv.at[sweep, 1],
            device_id=(me_s, me_c - 1), device_id_type=MESH)
        return right, left

    weights_right = pltpu.make_async_remote_copy(
        src_ref=stf.at[:, :, pl.ds(cols - LANES, LANES)], dst_ref=halo_w,
        send_sem=w_send, recv_sem=w_recv,
        device_id=(me_s, me_c + 1), device_id_type=MESH)

    def row_copy(number, step):
        return pltpu.make_async_remote_copy(
            src_ref=send_row.at[number], dst_ref=recv_row.at[number],
            send_sem=row_send.at[number], recv_sem=row_recv.at[number],
            device_id=(me_s + step, me_c), device_id_type=MESH)

    ups = [row_copy(t, -1) for t in range(ITERS)]
    downs = [row_copy(ITERS + t, 1) for t in range(ITERS + 1)]
    side = [side_copies(t) for t in range(ITERS)]

    row_of = lax.broadcasted_iota(jnp.int32, (SUB, cols), 0)
    field_row = lax.broadcasted_iota(jnp.int32, (rows, cols), 0)

    def compact(parts):
        total = jnp.zeros((SUB, cols), f32)
        for place, part in enumerate(parts):
            total = jnp.where(row_of == place, jnp.broadcast_to(part, (SUB, cols)), total)
        return total

    send_row[0] = compact([pos[c, 0:1] for c in range(3)])
    send_row[ITERS] = compact(
        [pos[c, rows - 1:rows] for c in range(3)] + [stf[1, rows - 1:rows]])

    @pl.when(jnp.logical_not(not_top))
    def _():
        for t in range(ITERS + 1):
            recv_row[ITERS + t] = jnp.zeros((SUB, cols), f32)

    @pl.when(jnp.logical_not(not_bottom))
    def _():
        for t in range(ITERS):
            recv_row[t] = jnp.zeros((SUB, cols), f32)

    @pl.when(jnp.logical_not(not_left))
    def _():
        halo_w[...] = jnp.zeros_like(halo_w)
        for t in range(ITERS):
            halo[t, 0] = jnp.zeros((3, rows, LANES), f32)

    @pl.when(jnp.logical_not(not_right))
    def _():
        for t in range(ITERS):
            halo[t, 1] = jnp.zeros((3, rows, LANES), f32)

    neighbours = sum(there.astype(jnp.int32) for there, _ in sides)
    pl.semaphore_wait(barrier, neighbours)

    @pl.when(not_right)
    def _():
        side[0][0].start()
        weights_right.start()

    @pl.when(not_left)
    def _():
        side[0][1].start()

    @pl.when(not_bottom)
    def _():
        downs[0].start()

    @pl.when(not_top)
    def _():
        ups[0].start()

    own_cols = lax.broadcasted_iota(jnp.int32, (1, cols), 1) + me_c * cols
    pinned = jnp.zeros((1, cols), jnp.int32)
    for number in range(pins.shape[0]):
        pinned = pinned | (own_cols == pins[number]).astype(jnp.int32)
    pinned = jnp.broadcast_to(pinned, (rows, cols)) * (field_row == 0) * jnp.where(not_top, 0, 1)
    inertial = [
        inertia[...] * tgt[c] + jnp.where(pinned > 0, pin_stiffness * pos[c], 0.0)
        for c in range(3)
    ]

    w_strip = [stf[1, srows * (k + 1) - 1:srows * (k + 1)] for k in range(strips)]
    eye = (
        lax.broadcasted_iota(jnp.int32, (cols, cols), 0)
        == lax.broadcasted_iota(jnp.int32, (cols, cols), 1)
    ).astype(f32).astype(bf16)
    product = None
    for k in range(strips):
        loads[k].wait()
        matrix = mats[k, last_start:, :cols]
        if k == 0:
            product = lax.dot_general(
                eye, matrix, (((1,), (1,)), ((), ())), preferred_element_type=f32)
        else:
            product = times_transposed(
                jnp.concatenate([high[k - 1], low[k - 1]], axis=0), matrix)
        if k < strips - 1:
            product = product * w_strip[k]
        upper = product.astype(bf16)
        high[k] = upper
        low[k] = (product - upper.astype(f32)).astype(bf16)

    wide = cols + 2 * LANES
    wide_lane = lax.broadcasted_iota(jnp.int32, (rows, wide), 1) - LANES
    wide_cols = wide_lane + me_c * cols
    grid_cols = n_col * cols
    vertical = jnp.where(field_row < rows - 1, stf[1], 0.0)
    is_last = field_row % srows == srows - 1
    w_down = jnp.where(is_last, vertical, 0.0)
    w_bottom = jnp.where(not_bottom, stf[1, rows - 1:rows], 0.0)
    rest_row = jnp.where(row_of == 1, 1.0, 0.0)

    def early_rhs(u, left, right, above, w_above):
        field = [jnp.concatenate([left[c], u[c], right[c]], axis=1) for c in range(3)]
        total = [jnp.zeros((rows, wide), f32)] * 3
        for number, offset in enumerate((1, 2)):
            ahead = [pltpu.roll(field[c], wide - offset, axis=1) for c in range(3)]
            gap = [ahead[c] - field[c] for c in range(3)]
            gap[0] = gap[0] + float(offset)
            scale = stretch(gap[0] * gap[0] + gap[1] * gap[1] + gap[2] * gap[2], float(offset))
            weight, cross = edge_w[number], cross_w[number]
            for c in range(3):
                moved = scale * gap[c]
                if c == 0:
                    moved = moved - float(offset)
                pull = weight * moved
                at_a = cross * ahead[c] - pull
                at_b = cross * field[c] + pull
                total[c] = total[c] + at_a + pltpu.roll(at_b, offset, axis=1)
        below = [pltpu.roll(u[c], rows - 1, axis=0) for c in range(3)]
        before = [
            jnp.where(field_row == 0, jnp.broadcast_to(above[c:c + 1], (rows, cols)),
                      pltpu.roll(u[c], 1, axis=0))
            for c in range(3)
        ]
        w_before = jnp.where(
            field_row == 0, jnp.broadcast_to(w_above, (rows, cols)),
            pltpu.roll(stf[1], 1, axis=0))
        gap = [below[c] - u[c] for c in range(3)]
        gap[1] = gap[1] + 1.0
        scale = stretch(gap[0] * gap[0] + gap[1] * gap[1] + gap[2] * gap[2], 1.0)
        back = [u[c] - before[c] for c in range(3)]
        back[1] = back[1] + 1.0
        back_scale = stretch(back[0] * back[0] + back[1] * back[1] + back[2] * back[2], 1.0)
        result = []
        for c in range(3):
            rest = 1.0 if c == 1 else 0.0
            value = inertial[c] + total[c][:, LANES:LANES + cols]
            value = value - vertical * (scale * gap[c] - rest) + w_down * below[c]
            result.append(value + w_before * (back_scale * back[c] - rest))
        return result

    def late_rhs(last_rows, below):
        gap = below - last_rows + rest_row
        scale = stretch(jnp.sum(gap * gap, axis=0, keepdims=True), 1.0)
        return w_bottom * (below - scale * gap + rest_row)

    def strip_vector(rhs, k):
        return [
            compact([rhs[c][srows * k + i:srows * k + i + 1] for c in range(3)])
            for i in range(srows)
        ]

    def receive(copy, there):
        @pl.when(there)
        def _():
            copy.wait_recv()

    def send(copy, there):
        @pl.when(there)
        def _():
            copy.start()

    @pl.when(not_left)
    def _():
        weights_right.wait_recv()

    for number, (offset, channel) in enumerate(((1, 0), (2, 2))):
        weight = jnp.concatenate(
            [halo_w[channel], stf[channel], jnp.zeros((rows, LANES), f32)], axis=1)
        inside = (wide_cols >= 0) & (wide_cols + offset <= grid_cols - 1)
        weight = jnp.where(inside, weight, 0.0)
        crossing = ((wide_lane < 0) & (wide_lane + offset >= 0)) | (
            (wide_lane < cols) & (wide_lane + offset >= cols))
        edge_w[number] = weight
        cross_w[number] = jnp.where(crossing, weight, 0.0)

    receive(downs[0], not_top)
    above = recv_row[ITERS]
    w_above = jnp.where(not_top, above[3:4], 0.0)
    current = [pos[c] for c in range(3)]
    last_rows = compact([pos[c, rows - 1:rows] for c in range(3)])

    for sweep in range(ITERS):
        receive(side[sweep][0], not_left)
        receive(side[sweep][1], not_right)
        rhs = early_rhs(
            current, [halo[sweep, 0, c] for c in range(3)], [halo[sweep, 1, c] for c in range(3)],
            above, w_above)
        vectors = [strip_vector(rhs, k) for k in range(strips)]
        if sweep == 0:
            receive(ups[sweep], not_bottom)
            vectors[-1][-1] = vectors[-1][-1] + late_rhs(last_rows, recv_row[sweep])
        base, offsets = [], []
        for k in range(strips):
            parts = split(jnp.concatenate(vectors[k], axis=1))
            base.append(times_transposed(parts, mats[k]))
        carried = None
        for k in range(strips):
            if k == 0:
                carried = base[k][:, last_start:]
            else:
                carried = base[k][:, last_start:] + times_transposed(
                    split(carried), mats[k, last_start:, :cols])
            if k < strips - 1:
                carried = carried * w_strip[k]
            offsets.append(carried)
        if sweep > 0:
            receive(ups[sweep], not_bottom)
            late = split(late_rhs(last_rows, recv_row[sweep]))
            change = times_transposed(late, mats[strips - 1, :, last_start:])
            base[-1] = base[-1] + change
            offsets[-1] = offsets[-1] + change[:, last_start:]

        receive(downs[sweep + 1], not_top)
        above = recv_row[ITERS + sweep + 1]
        entering = split(above * w_above)
        last_rows = offsets[-1] + times_pair(entering, high[strips - 1], low[strips - 1])
        send_row[ITERS + sweep + 1] = last_rows
        send(downs[sweep + 1], not_bottom)
        solved = [base[0] + times_transposed(entering, mats[0, :, :cols])]
        if sweep < ITERS - 1:
            send_row[sweep + 1] = solved[0][:, :cols]
            send(ups[sweep + 1], not_top)
        for k in range(1, strips):
            carried = offsets[k - 1] + times_pair(entering, high[k - 1], low[k - 1])
            solved.append(base[k] + times_transposed(split(carried), mats[k, :, :cols]))
        current = []
        for c in range(3):
            field = jnp.zeros((rows, cols), f32)
            for k in range(strips):
                for i in range(srows):
                    row = solved[k][c:c + 1, i * cols:(i + 1) * cols]
                    field = jnp.where(
                        field_row == srows * k + i, jnp.broadcast_to(row, (rows, cols)), field)
            current.append(field)
            if sweep < ITERS - 1:
                disp[c] = field
            else:
                out[c] = field
        if sweep < ITERS - 1:
            send(side[sweep + 1][0], not_right)
            send(side[sweep + 1][1], not_left)

    def sent(copy, there):
        @pl.when(there)
        def _():
            copy.wait_send()

    sent(weights_right, not_right)
    for right, left in side:
        sent(right, not_right)
        sent(left, not_left)
    for copy in ups:
        sent(copy, not_top)
    for copy in downs:
        sent(copy, not_bottom)


def shards(n_strip, n_col, positions, target, inertia, stiffness, pin_columns, inverses):
    rows, cols = positions.shape[1:]
    strips, block, _ = inverses.shape
    vmem = pl.BlockSpec(memory_space=pltpu.VMEM)
    dma = pltpu.SemaphoreType.DMA
    return pl.pallas_call(
        functools.partial(kernel, n_strip, n_col),
        out_shape=jax.ShapeDtypeStruct(positions.shape, f32),
        in_specs=[pl.BlockSpec(memory_space=pltpu.SMEM)] + [vmem] * 4
        + [pl.BlockSpec(memory_space=pl.ANY)],
        out_specs=vmem,
        scratch_shapes=[
            pltpu.VMEM(inverses.shape, bf16),
            pltpu.VMEM((strips, cols, cols), bf16),
            pltpu.VMEM((strips, cols, cols), bf16),
            pltpu.VMEM(positions.shape, f32),
            pltpu.VMEM((ITERS, 2, 3, rows, LANES), f32),
            pltpu.VMEM((3, rows, LANES), f32),
            pltpu.VMEM((2 * ITERS + 1, SUB, cols), f32),
            pltpu.VMEM((2 * ITERS + 1, SUB, cols), f32),
            pltpu.VMEM((2, rows, cols + 2 * LANES), f32),
            pltpu.VMEM((2, rows, cols + 2 * LANES), f32),
            dma((strips,)),
            dma((ITERS, 2)),
            dma((ITERS, 2)),
            dma,
            dma,
            dma((2 * ITERS + 1,)),
            dma((2 * ITERS + 1,)),
        ],
        compiler_params=pltpu.CompilerParams(
            collective_id=0, has_side_effects=True, vmem_limit_bytes=32 * 1024 * 1024),
    )(pin_columns, positions, target, inertia, stiffness, inverses)


def solution(mesh):
    in_specs = (
        P(None, "strip", "col"),
        P(None, "strip", "col"),
        P("strip", "col"),
        P(None, "strip", "col"),
        P(),
        P("strip", None, None),
    )
    out_specs = P(None, "strip", "col")
    run = functools.partial(shards, mesh.shape["strip"], mesh.shape["col"])
    return jax.shard_map(run, mesh=mesh, in_specs=in_specs, out_specs=out_specs, check_vma=False)
```

time: 144 us -> 39.4 us (0.27)
  the two profiles are of different devices: /device:TPU:24 before, /device:TPU:30 now
where the time goes in v1:
time: 39.4 us; the launch traced here: 39 us
  Pallas kernels  33.3 us (85%)
  local copies, waits for them, and re-layouts  5.76 us (15%)
    pallas_call x1, Pallas kernels, shards(): pl.pallas_call(functools.partial(kernel, n_strip, n_col), out_shape=jax.S...  33.3 us
    unnamed x13, local copies, waits for them, and re-layouts  5.76 us

profile of v1, /device:TPU:30, one launch (start us, length us, event | category | flops | bytes accessed | tf_op | source)
XLA Modules:
  0.0 39.0 jit_solution(2012287809310789883)
XLA Ops:
  0.0 0.0 copy-start
  0.0 1.6 %copy-done = bf16[4,512,512]{2,1,0:T(8,128)(2,1)S(1)} copy-done((bf16[4,512,512]{2,1,0:T(8,128)(2,1)S(1)}, bf16[4,512,512]{2,1,0:T(8,128)(2,1)}, u32[]{:S(2)}) %copy-start) | copy-done | bytes 2097176
  1.6 0.0 copy-start.1
  1.6 0.7 %copy-done.1 = f32[3,8,256]{2,1,0:T(8,128)S(1)} copy-done((f32[3,8,256]{2,1,0:T(8,128)S(1)}, f32[3,8,256]{2,1,0:T(8,128)}, u32[]{:S(2)}) %copy-start.1) | copy-done | bytes 24600
  2.3 0.0 copy-start.2
  2.3 0.7 %copy-done.2 = f32[3,8,256]{2,1,0:T(8,128)S(1)} copy-done((f32[3,8,256]{2,1,0:T(8,128)S(1)}, f32[3,8,256]{2,1,0:T(8,128)}, u32[]{:S(2)}) %copy-start.2) | copy-done | bytes 24600
  3.1 0.0 copy-start.3
  3.1 0.7 %copy-done.3 = f32[3,8,256]{2,1,0:T(8,128)S(1)} copy-done((f32[3,8,256]{2,1,0:T(8,128)S(1)}, f32[3,8,256]{2,1,0:T(8,128)}, u32[]{:S(2)}) %copy-start.3) | copy-done | bytes 24600
  3.8 0.0 copy-start.4
  3.8 0.7 %copy-done.4 = f32[8,256]{1,0:T(8,128)S(1)} copy-done((f32[8,256]{1,0:T(8,128)S(1)}, f32[8,256]{1,0:T(8,128)}, u32[]{:S(2)}) %copy-start.4) | copy-done | bytes 8216
  4.5 0.0 copy-start.5
  4.5 0.7 %copy-done.5 = s32[64]{0:T(128)S(1)} copy-done((s32[64]{0:T(128)S(1)}, s32[64]{0:T(128)}, u32[]{:S(2)}) %copy-start.5) | copy-done | bytes 280
  5.2 33.3 %shard_map.64 = f32[3,8,256]{2,1,0:T(8,128)S(1)} custom-call(s32[64]{0:T(128)S(1)} %copy-done.5, f32[3,8,256]{2,1,0:T(8,128)S(1)} %copy-done.1, f32[3,8,256]{2,1,0:T(8,128)S(1)} %copy-done.2, f32[8,256]{1,0:T(8,128)S(1)} %copy-done.4, f32[3,8,256]{2,1,0:T(8,128)S(1)} %copy-done.3, bf16[4,512,512]{2,1,0:T(8,128)(2,1)S(1)} %copy-done), custom_call_target="tpu_custom_call" | custom-call | tf_op jit(solution)/shard_map/pallas_call | solution.py:366
  38.4 0.6 %copy.8 = f32[3,8,256]{2,1,0:T(8,128)} copy(f32[3,8,256]{2,1,0:T(8,128)S(1)} %shard_map.64) | data formatting | bytes 49152
Async XLA Ops:
  0.0 1.6 %copy-start = (bf16[4,512,512]{2,1,0:T(8,128)(2,1)S(1)}, bf16[4,512,512]{2,1,0:T(8,128)(2,1)}, u32[]{:S(2)}) copy-start(bf16[4,512,512]{2,1,0:T(8,128)(2,1)} %inv.1) | copy-start | bytes 6291460
  1.6 0.7 %copy-start.1 = (f32[3,8,256]{2,1,0:T(8,128)S(1)}, f32[3,8,256]{2,1,0:T(8,128)}, u32[]{:S(2)}) copy-start(f32[3,8,256]{2,1,0:T(8,128)} %pos.1) | copy-start | bytes 73732
  2.3 0.7 %copy-start.2 = (f32[3,8,256]{2,1,0:T(8,128)S(1)}, f32[3,8,256]{2,1,0:T(8,128)}, u32[]{:S(2)}) copy-start(f32[3,8,256]{2,1,0:T(8,128)} %tgt.1) | copy-start | bytes 73732
  3.1 0.7 %copy-start.3 = (f32[3,8,256]{2,1,0:T(8,128)S(1)}, f32[3,8,256]{2,1,0:T(8,128)}, u32[]{:S(2)}) copy-start(f32[3,8,256]{2,1,0:T(8,128)} %stf.1) | copy-start | bytes 73732
  3.8 0.7 %copy-start.4 = (f32[8,256]{1,0:T(8,128)S(1)}, f32[8,256]{1,0:T(8,128)}, u32[]{:S(2)}) copy-start(f32[8,256]{1,0:T(8,128)} %inertia.1) | copy-start | bytes 24580
  4.5 0.7 %copy-start.5 = (s32[64]{0:T(128)S(1)}, s32[64]{0:T(128)}, u32[]{:S(2)}) copy-start(s32[64]{0:T(128)} %pins.1) | copy-start | bytes 772

commit v2 on v1

--- a/solution.py
+++ b/solution.py
@@ -16,8 +16,6 @@
 f32 = jnp.float32
 bf16 = jnp.bfloat16
 
-TO_RIGHT, TO_LEFT, UP, DOWN = range(4)
-
 
 def split(v):
     high = v.astype(bf16).astype(f32)
@@ -49,10 +47,12 @@
 
 def kernel(
     n_strip, n_col,
-    pins, pos, tgt, inertia, stf, inv,
+    pins_in, pos_in, tgt_in, inertia_in, stf_in, inv,
     out,
+    pins, pos, tgt, inertia, stf,
     mats, high, low, disp, halo, halo_w, send_row, recv_row, edge_w, cross_w,
-    inv_sem, side_send, side_recv, w_send, w_recv, row_send, row_recv,
+    map_send, map_recv, map_high, map_low, both_high, both_low, above_row,
+    in_sem, inv_sem, side_send, side_recv, w_send, w_recv, row_send, row_recv, m_send, m_recv,
 ):
     rows, cols = pos.shape[1], pos.shape[2]
     strips = inv.shape[0]
@@ -63,6 +63,19 @@
     not_top, not_bottom = me_s > 0, me_s < n_strip - 1
     not_left, not_right = me_c > 0, me_c < n_col - 1
 
+    is_tail, is_lead = me_s % 2 == 1, me_s % 2 == 0
+    tail_after = is_tail & (me_s + 2 < n_strip)
+    tail_before = is_tail & (me_s >= 2)
+    lead_before = is_lead & not_top
+    mapped_lead = lead_before & not_bottom
+
+    fetches = [
+        pltpu.make_async_copy(source, target, in_sem.at[number])
+        for number, (source, target) in enumerate((
+            (pos_in, pos), (stf_in, stf), (pins_in, pins), (tgt_in, tgt), (inertia_in, inertia)))
+    ]
+    for fetch in fetches:
+        fetch.start()
     loads = [pltpu.make_async_copy(inv.at[k], mats.at[k], inv_sem.at[k]) for k in range(strips)]
     for load in loads:
         load.start()
@@ -73,6 +86,8 @@
         (not_bottom, (me_s + 1, me_c)),
         (not_left, (me_s, me_c - 1)),
         (not_right, (me_s, me_c + 1)),
+        (tail_before, (me_s - 2, me_c)),
+        (tail_after, (me_s + 2, me_c)),
     )
     for there, device in sides:
         @pl.when(there)
@@ -103,7 +118,14 @@
             device_id=(me_s + step, me_c), device_id_type=MESH)
 
     ups = [row_copy(t, -1) for t in range(ITERS)]
-    downs = [row_copy(ITERS + t, 1) for t in range(ITERS + 1)]
+    first_down = row_copy(ITERS, 1)
+    base_row = ITERS + 1
+    lead_out = [row_copy(base_row + t, 1) for t in range(ITERS)]
+    tail_out = [row_copy(base_row + ITERS + t, 2) for t in range(ITERS)]
+    next_out = [row_copy(base_row + 2 * ITERS + t, 1) for t in range(ITERS)]
+    map_copy = pltpu.make_async_remote_copy(
+        src_ref=map_send, dst_ref=map_recv, send_sem=m_send, recv_sem=m_recv,
+        device_id=(me_s + 1, me_c), device_id_type=MESH)
     side = [side_copies(t) for t in range(ITERS)]
 
     row_of = lax.broadcasted_iota(jnp.int32, (SUB, cols), 0)
@@ -115,14 +137,15 @@
             total = jnp.where(row_of == place, jnp.broadcast_to(part, (SUB, cols)), total)
         return total
 
+    fetches[0].wait()
+    fetches[1].wait()
     send_row[0] = compact([pos[c, 0:1] for c in range(3)])
     send_row[ITERS] = compact(
         [pos[c, rows - 1:rows] for c in range(3)] + [stf[1, rows - 1:rows]])
 
     @pl.when(jnp.logical_not(not_top))
     def _():
-        for t in range(ITERS + 1):
-            recv_row[ITERS + t] = jnp.zeros((SUB, cols), f32)
+        recv_row[ITERS] = jnp.zeros((SUB, cols), f32)
 
     @pl.when(jnp.logical_not(not_bottom))
     def _():
@@ -140,26 +163,8 @@
         for t in range(ITERS):
             halo[t, 1] = jnp.zeros((3, rows, LANES), f32)
 
-    neighbours = sum(there.astype(jnp.int32) for there, _ in sides)
-    pl.semaphore_wait(barrier, neighbours)
-
-    @pl.when(not_right)
-    def _():
-        side[0][0].start()
-        weights_right.start()
-
-    @pl.when(not_left)
-    def _():
-        side[0][1].start()
-
-    @pl.when(not_bottom)
-    def _():
-        downs[0].start()
-
-    @pl.when(not_top)
-    def _():
-        ups[0].start()
-
+    for fetch in fetches[2:]:
+        fetch.wait()
     own_cols = lax.broadcasted_iota(jnp.int32, (1, cols), 1) + me_c * cols
     pinned = jnp.zeros((1, cols), jnp.int32)
     for number in range(pins.shape[0]):
@@ -169,6 +174,26 @@
         inertia[...] * tgt[c] + jnp.where(pinned > 0, pin_stiffness * pos[c], 0.0)
         for c in range(3)
     ]
+
+    neighbours = sum(there.astype(jnp.int32) for there, _ in sides)
+    pl.semaphore_wait(barrier, neighbours)
+
+    @pl.when(not_right)
+    def _():
+        side[0][0].start()
+        weights_right.start()
+
+    @pl.when(not_left)
+    def _():
+        side[0][1].start()
+
+    @pl.when(not_bottom)
+    def _():
+        first_down.start()
+
+    @pl.when(not_top)
+    def _():
+        ups[0].start()
 
     w_strip = [stf[1, srows * (k + 1) - 1:srows * (k + 1)] for k in range(strips)]
     eye = (
@@ -187,6 +212,12 @@
                 jnp.concatenate([high[k - 1], low[k - 1]], axis=0), matrix)
         if k < strips - 1:
             product = product * w_strip[k]
+        else:
+            map_send[...] = product
+
+            @pl.when(mapped_lead)
+            def _():
+                map_copy.start()
         upper = product.astype(bf16)
         high[k] = upper
         low[k] = (product - upper.astype(f32)).astype(bf16)
@@ -276,7 +307,7 @@
         edge_w[number] = weight
         cross_w[number] = jnp.where(crossing, weight, 0.0)
 
-    receive(downs[0], not_top)
+    receive(first_down, not_top)
     above = recv_row[ITERS]
     w_above = jnp.where(not_top, above[3:4], 0.0)
     current = [pos[c] for c in range(3)]
@@ -313,12 +344,56 @@
             base[-1] = base[-1] + change
             offsets[-1] = offsets[-1] + change[:, last_start:]
 
-        receive(downs[sweep + 1], not_top)
-        above = recv_row[ITERS + sweep + 1]
+        send_row[base_row + sweep] = offsets[-1]
+        send(lead_out[sweep], is_lead & not_bottom)
+
+        def pass_on(tail_rows):
+            send_row[base_row + ITERS + sweep] = tail_rows * w_bottom
+            send_row[base_row + 2 * ITERS + sweep] = tail_rows
+            send(tail_out[sweep], tail_after)
+            send(next_out[sweep], is_tail & not_bottom)
+
+        @pl.when(is_tail)
+        def _():
+            lead_out[sweep].wait_recv()
+            lead_rows = recv_row[base_row + sweep]
+            tail_rows = offsets[-1] + times_pair(
+                split(lead_rows * w_above), high[strips - 1], low[strips - 1])
+
+            @pl.when(jnp.logical_not(tail_before))
+            def _():
+                pass_on(tail_rows)
+                above_row[...] = lead_rows
+
+            @pl.when(tail_before)
+            def _():
+                if sweep == 0:
+                    map_copy.wait_recv()
+                    received = map_recv[...]
+                    upper = received.astype(bf16)
+                    map_high[...] = upper
+                    map_low[...] = (received - upper.astype(f32)).astype(bf16)
+                    both = times_pair(
+                        split(received * w_above), high[strips - 1], low[strips - 1])
+                    upper = both.astype(bf16)
+                    both_high[...] = upper
+                    both_low[...] = (both - upper.astype(f32)).astype(bf16)
+                tail_out[sweep].wait_recv()
+                entering = split(recv_row[base_row + ITERS + sweep])
+                pass_on(tail_rows + times_pair(entering, both_high[...], both_low[...]))
+                above_row[...] = lead_rows + times_pair(entering, map_high[...], map_low[...])
+
+        @pl.when(lead_before)
+        def _():
+            next_out[sweep].wait_recv()
+            above_row[...] = recv_row[base_row + 2 * ITERS + sweep]
+
+        @pl.when(jnp.logical_not(not_top))
+        def _():
+            above_row[...] = jnp.zeros((SUB, cols), f32)
+
+        above = above_row[...]
         entering = split(above * w_above)
-        last_rows = offsets[-1] + times_pair(entering, high[strips - 1], low[strips - 1])
-        send_row[ITERS + sweep + 1] = last_rows
-        send(downs[sweep + 1], not_bottom)
         solved = [base[0] + times_transposed(entering, mats[0, :, :cols])]
         if sweep < ITERS - 1:
             send_row[sweep + 1] = solved[0][:, :cols]
@@ -326,6 +401,7 @@
         for k in range(1, strips):
             carried = offsets[k - 1] + times_pair(entering, high[k - 1], low[k - 1])
             solved.append(base[k] + times_transposed(split(carried), mats[k, :, :cols]))
+        last_rows = solved[-1][:, last_start:]
         current = []
         for c in range(3):
             field = jnp.zeros((rows, cols), f32)
@@ -354,39 +430,57 @@
         sent(left, not_left)
     for copy in ups:
         sent(copy, not_top)
-    for copy in downs:
-        sent(copy, not_bottom)
+    sent(first_down, not_bottom)
+    sent(map_copy, mapped_lead)
+    for t in range(ITERS):
+        sent(lead_out[t], is_lead & not_bottom)
+        sent(tail_out[t], tail_after)
+        sent(next_out[t], is_tail & not_bottom)
 
 
 def shards(n_strip, n_col, positions, target, inertia, stiffness, pin_columns, inverses):
     rows, cols = positions.shape[1:]
     strips, block, _ = inverses.shape
-    vmem = pl.BlockSpec(memory_space=pltpu.VMEM)
+    messages = 4 * ITERS + 1
     dma = pltpu.SemaphoreType.DMA
     return pl.pallas_call(
         functools.partial(kernel, n_strip, n_col),
         out_shape=jax.ShapeDtypeStruct(positions.shape, f32),
-        in_specs=[pl.BlockSpec(memory_space=pltpu.SMEM)] + [vmem] * 4
-        + [pl.BlockSpec(memory_space=pl.ANY)],
-        out_specs=vmem,
+        in_specs=[pl.BlockSpec(memory_space=pltpu.HBM)] * 6,
+        out_specs=pl.BlockSpec(memory_space=pltpu.VMEM),
         scratch_shapes=[
+            pltpu.SMEM(pin_columns.shape, jnp.int32),
+            pltpu.VMEM(positions.shape, f32),
+            pltpu.VMEM(target.shape, f32),
+            pltpu.VMEM(inertia.shape, f32),
+            pltpu.VMEM(stiffness.shape, f32),
             pltpu.VMEM(inverses.shape, bf16),
             pltpu.VMEM((strips, cols, cols), bf16),
             pltpu.VMEM((strips, cols, cols), bf16),
             pltpu.VMEM(positions.shape, f32),
             pltpu.VMEM((ITERS, 2, 3, rows, LANES), f32),
             pltpu.VMEM((3, rows, LANES), f32),
-            pltpu.VMEM((2 * ITERS + 1, SUB, cols), f32),
-            pltpu.VMEM((2 * ITERS + 1, SUB, cols), f32),
+            pltpu.VMEM((messages, SUB, cols), f32),
+            pltpu.VMEM((messages, SUB, cols), f32),
             pltpu.VMEM((2, rows, cols + 2 * LANES), f32),
             pltpu.VMEM((2, rows, cols + 2 * LANES), f32),
+            pltpu.VMEM((cols, cols), f32),
+            pltpu.VMEM((cols, cols), f32),
+            pltpu.VMEM((cols, cols), bf16),
+            pltpu.VMEM((cols, cols), bf16),
+            pltpu.VMEM((cols, cols), bf16),
+            pltpu.VMEM((cols, cols), bf16),
+            pltpu.VMEM((SUB, cols), f32),
+            dma((5,)),
             dma((strips,)),
             dma((ITERS, 2)),
             dma((ITERS, 2)),
             dma,
             dma,
-            dma((2 * ITERS + 1,)),
-            dma((2 * ITERS + 1,)),
+            dma((messages,)),
+            dma((messages,)),
+            dma,
+            dma,
         ],
         compiler_params=pltpu.CompilerParams(
             collective_id=0, has_side_effects=True, vmem_limit_bytes=32 * 1024 * 1024),

time: 39.4 us -> 30.7 us (0.78)
  the two profiles are of different devices: /device:TPU:30 before, /device:TPU:24 now
where the time goes in v2:
time: 30.7 us; the launch traced here: 30.3 us
  Pallas kernels  24.5 us (80%)
  local copies, waits for them, and re-layouts  5.76 us (19%)
    pallas_call x1, Pallas kernels, shards(): pl.pallas_call(functools.partial(kernel, n_strip, n_col), out_shape=jax.S...  24.5 us
    unnamed x13, local copies, waits for them, and re-layouts  5.76 us

profile of v2, /device:TPU:24, one launch (start us, length us, event | category | flops | bytes accessed | tf_op | source)
XLA Modules:
  0.0 30.3 jit_solution(16174310673084776536)
XLA Ops:
  0.0 0.0 copy-start
  0.0 1.6 %copy-done = bf16[4,512,512]{2,1,0:T(8,128)(2,1)S(1)} copy-done((bf16[4,512,512]{2,1,0:T(8,128)(2,1)S(1)}, bf16[4,512,512]{2,1,0:T(8,128)(2,1)}, u32[]{:S(2)}) %copy-start) | copy-done | bytes 2097176
  1.6 0.0 copy-start.1
  1.6 0.7 %copy-done.1 = f32[3,8,256]{2,1,0:T(8,128)S(1)} copy-done((f32[3,8,256]{2,1,0:T(8,128)S(1)}, f32[3,8,256]{2,1,0:T(8,128)}, u32[]{:S(2)}) %copy-start.1) | copy-done | bytes 24600
  2.3 0.0 copy-start.2
  2.3 0.7 %copy-done.2 = f32[3,8,256]{2,1,0:T(8,128)S(1)} copy-done((f32[3,8,256]{2,1,0:T(8,128)S(1)}, f32[3,8,256]{2,1,0:T(8,128)}, u32[]{:S(2)}) %copy-start.2) | copy-done | bytes 24600
  3.1 0.0 copy-start.3
  3.1 0.7 %copy-done.3 = f32[3,8,256]{2,1,0:T(8,128)S(1)} copy-done((f32[3,8,256]{2,1,0:T(8,128)S(1)}, f32[3,8,256]{2,1,0:T(8,128)}, u32[]{:S(2)}) %copy-start.3) | copy-done | bytes 24600
  3.8 0.0 copy-start.4
  3.8 0.7 %copy-done.4 = f32[8,256]{1,0:T(8,128)S(1)} copy-done((f32[8,256]{1,0:T(8,128)S(1)}, f32[8,256]{1,0:T(8,128)}, u32[]{:S(2)}) %copy-start.4) | copy-done | bytes 8216
  4.5 0.0 copy-start.5
  4.5 0.7 %copy-done.5 = s32[64]{0:T(128)S(1)} copy-done((s32[64]{0:T(128)S(1)}, s32[64]{0:T(128)}, u32[]{:S(2)}) %copy-start.5) | copy-done | bytes 280
  5.2 24.5 %shard_map.64 = f32[3,8,256]{2,1,0:T(8,128)S(1)} custom-call(s32[64]{0:T(128)S(1)} %copy-done.5, f32[3,8,256]{2,1,0:T(8,128)S(1)} %copy-done.1, f32[3,8,256]{2,1,0:T(8,128)S(1)} %copy-done.2, f32[8,256]{1,0:T(8,128)S(1)} %copy-done.4, f32[3,8,256]{2,1,0:T(8,128)S(1)} %copy-done.3, bf16[4,512,512]{2,1,0:T(8,128)(2,1)S(1)} %copy-done), custom_call_target="tpu_custom_call" | custom-call | tf_op jit(solution)/shard_map/pallas_call | solution.py:446
  29.7 0.6 %copy.8 = f32[3,8,256]{2,1,0:T(8,128)} copy(f32[3,8,256]{2,1,0:T(8,128)S(1)} %shard_map.64) | data formatting | bytes 49152
Async XLA Ops:
  0.0 1.6 %copy-start = (bf16[4,512,512]{2,1,0:T(8,128)(2,1)S(1)}, bf16[4,512,512]{2,1,0:T(8,128)(2,1)}, u32[]{:S(2)}) copy-start(bf16[4,512,512]{2,1,0:T(8,128)(2,1)} %inv.1) | copy-start | bytes 6291460
  1.6 0.7 %copy-start.1 = (f32[3,8,256]{2,1,0:T(8,128)S(1)}, f32[3,8,256]{2,1,0:T(8,128)}, u32[]{:S(2)}) copy-start(f32[3,8,256]{2,1,0:T(8,128)} %pos_in.1) | copy-start | bytes 73732
  2.3 0.7 %copy-start.2 = (f32[3,8,256]{2,1,0:T(8,128)S(1)}, f32[3,8,256]{2,1,0:T(8,128)}, u32[]{:S(2)}) copy-start(f32[3,8,256]{2,1,0:T(8,128)} %tgt_in.1) | copy-start | bytes 73732
  3.1 0.7 %copy-start.3 = (f32[3,8,256]{2,1,0:T(8,128)S(1)}, f32[3,8,256]{2,1,0:T(8,128)}, u32[]{:S(2)}) copy-start(f32[3,8,256]{2,1,0:T(8,128)} %stf_in.1) | copy-start | bytes 73732
  3.8 0.7 %copy-start.4 = (f32[8,256]{1,0:T(8,128)S(1)}, f32[8,256]{1,0:T(8,128)}, u32[]{:S(2)}) copy-start(f32[8,256]{1,0:T(8,128)} %inertia_in.1) | copy-start | bytes 24580
  4.5 0.7 %copy-start.5 = (s32[64]{0:T(128)S(1)}, s32[64]{0:T(128)}, u32[]{:S(2)}) copy-start(s32[64]{0:T(128)} %pins_in.1) | copy-start | bytes 772

commit v3 on v2

--- a/solution.py
+++ b/solution.py
@@ -163,6 +163,58 @@
         for t in range(ITERS):
             halo[t, 1] = jnp.zeros((3, rows, LANES), f32)
 
+    w_strip = [stf[1, srows * (k + 1) - 1:srows * (k + 1)] for k in range(strips)]
+
+    def extend_product(first, after):
+        for k in range(first, after):
+            loads[k].wait()
+            matrix = mats[k, last_start:, :cols]
+            if k == 0:
+                eye = (
+                    lax.broadcasted_iota(jnp.int32, (cols, cols), 0)
+                    == lax.broadcasted_iota(jnp.int32, (cols, cols), 1)
+                ).astype(f32).astype(bf16)
+                product = lax.dot_general(
+                    eye, matrix, (((1,), (1,)), ((), ())), preferred_element_type=f32)
+            else:
+                product = times_transposed(
+                    jnp.concatenate([high[k - 1], low[k - 1]], axis=0), matrix)
+            if k < strips - 1:
+                product = product * w_strip[k]
+            else:
+                map_send[...] = product
+
+                @pl.when(mapped_lead)
+                def _():
+                    map_copy.start()
+            upper = product.astype(bf16)
+            high[k] = upper
+            low[k] = (product - upper.astype(f32)).astype(bf16)
+
+    extend_product(0, strips // 2)
+
+    neighbours = sum(there.astype(jnp.int32) for there, _ in sides)
+    pl.semaphore_wait(barrier, neighbours)
+
+    @pl.when(not_right)
+    def _():
+        side[0][0].start()
+        weights_right.start()
+
+    @pl.when(not_left)
+    def _():
+        side[0][1].start()
+
+    @pl.when(not_bottom)
+    def _():
+        first_down.start()
+
+    @pl.when(not_top)
+    def _():
+        ups[0].start()
+
+    extend_product(strips // 2, strips)
+
     for fetch in fetches[2:]:
         fetch.wait()
     own_cols = lax.broadcasted_iota(jnp.int32, (1, cols), 1) + me_c * cols
@@ -174,53 +226,6 @@
         inertia[...] * tgt[c] + jnp.where(pinned > 0, pin_stiffness * pos[c], 0.0)
         for c in range(3)
     ]
-
-    neighbours = sum(there.astype(jnp.int32) for there, _ in sides)
-    pl.semaphore_wait(barrier, neighbours)
-
-    @pl.when(not_right)
-    def _():
-        side[0][0].start()
-        weights_right.start()
-
-    @pl.when(not_left)
-    def _():
-        side[0][1].start()
-
-    @pl.when(not_bottom)
-    def _():
-        first_down.start()
-
-    @pl.when(not_top)
-    def _():
-        ups[0].start()
-
-    w_strip = [stf[1, srows * (k + 1) - 1:srows * (k + 1)] for k in range(strips)]
-    eye = (
-        lax.broadcasted_iota(jnp.int32, (cols, cols), 0)
-        == lax.broadcasted_iota(jnp.int32, (cols, cols), 1)
-    ).astype(f32).astype(bf16)
-    product = None
-    for k in range(strips):
-        loads[k].wait()
-        matrix = mats[k, last_start:, :cols]
-        if k == 0:
-            product = lax.dot_general(
-                eye, matrix, (((1,), (1,)), ((), ())), preferred_element_type=f32)
-        else:
-            product = times_transposed(
-                jnp.concatenate([high[k - 1], low[k - 1]], axis=0), matrix)
-        if k < strips - 1:
-            product = product * w_strip[k]
-        else:
-            map_send[...] = product
-
-            @pl.when(mapped_lead)
-            def _():
-                map_copy.start()
-        upper = product.astype(bf16)
-        high[k] = upper
-        low[k] = (product - upper.astype(f32)).astype(bf16)
 
     wide = cols + 2 * LANES
     wide_lane = lax.broadcasted_iota(jnp.int32, (rows, wide), 1) - LANES
@@ -483,7 +488,7 @@
             dma,
         ],
         compiler_params=pltpu.CompilerParams(
-            collective_id=0, has_side_effects=True, vmem_limit_bytes=32 * 1024 * 1024),
+            collective_id=0, has_side_effects=True, vmem_limit_bytes=67_000_000),
     )(pin_columns, positions, target, inertia, stiffness, inverses)
 
 

time: 30.7 us -> 26.1 us (0.85)
  local copies, waits for them, and re-layouts: 5.76 us -> 1.35 us
    unnamed x13 -> x1, local copies, waits for them, and re-layouts: 5.76 us -> 1.35 us
where the time goes in v3:
time: 26.1 us; the launch traced here: 25.9 us
  Pallas kernels  24.5 us (94%)
  local copies, waits for them, and re-layouts  1.35 us (5%)
    pallas_call x1, Pallas kernels, shards(): pl.pallas_call(functools.partial(kernel, n_strip, n_col), out_shape=jax.S...  24.5 us
    unnamed x1, local copies, waits for them, and re-layouts  1.35 us

profile of v3, /device:TPU:24, one launch (start us, length us, event | category | flops | bytes accessed | tf_op | source)
XLA Modules:
  0.0 25.9 jit_solution(1230993454477455945)
XLA Ops:
  0.0 24.5 %shard_map.64 = f32[3,8,256]{2,1,0:T(8,128)} custom-call(s32[64]{0:T(128)} %pins_in.1, f32[3,8,256]{2,1,0:T(8,128)} %pos_in.1, f32[3,8,256]{2,1,0:T(8,128)} %tgt_in.1, f32[8,256]{1,0:T(8,128)} %inertia_in.1, f32[3,8,256]{2,1,0:T(8,128)} %stf_in.1, bf16[4,512,512]{2,1,0:T(8,128)(2,1)} %inv.1), custom_call_target="tpu_custom_call" | custom-call | tf_op jit(solution)/shard_map/pallas_call | solution.py:451
  24.5 1.3 %copy.8 = f32[3,8,256]{2,1,0:T(8,128)} copy(f32[3,8,256]{2,1,0:T(8,128)} %shard_map.64) | data formatting | bytes 49152

commit v4 on v3

--- a/solution.py
+++ b/solution.py
@@ -51,7 +51,7 @@
     out,
     pins, pos, tgt, inertia, stf,
     mats, high, low, disp, halo, halo_w, send_row, recv_row, edge_w, cross_w,
-    map_send, map_recv, map_high, map_low, both_high, both_low, above_row,
+    map_send, map_recv, map_high, map_low, both_high, both_low, above_row, late_change,
     in_sem, inv_sem, side_send, side_recv, w_send, w_recv, row_send, row_recv, m_send, m_recv,
 ):
     rows, cols = pos.shape[1], pos.shape[2]
@@ -149,6 +149,7 @@
 
     @pl.when(jnp.logical_not(not_bottom))
     def _():
+        late_change[...] = jnp.zeros_like(late_change)
         for t in range(ITERS):
             recv_row[t] = jnp.zeros((SUB, cols), f32)
 
@@ -342,15 +343,19 @@
             if k < strips - 1:
                 carried = carried * w_strip[k]
             offsets.append(carried)
-        if sweep > 0:
-            receive(ups[sweep], not_bottom)
+        def add_late():
+            if sweep == 0:
+                return 0.0
+            ups[sweep].wait_recv()
             late = split(late_rhs(last_rows, recv_row[sweep]))
             change = times_transposed(late, mats[strips - 1, :, last_start:])
-            base[-1] = base[-1] + change
-            offsets[-1] = offsets[-1] + change[:, last_start:]
-
-        send_row[base_row + sweep] = offsets[-1]
-        send(lead_out[sweep], is_lead & not_bottom)
+            late_change[...] = change
+            return change[:, last_start:]
+
+        @pl.when(is_lead & not_bottom)
+        def _():
+            send_row[base_row + sweep] = offsets[-1] + add_late()
+            lead_out[sweep].start()
 
         def pass_on(tail_rows):
             send_row[base_row + ITERS + sweep] = tail_rows * w_bottom
@@ -367,7 +372,10 @@
 
             @pl.when(jnp.logical_not(tail_before))
             def _():
-                pass_on(tail_rows)
+                @pl.when(not_bottom)
+                def _():
+                    pass_on(tail_rows + add_late())
+
                 above_row[...] = lead_rows
 
             @pl.when(tail_before)
@@ -385,7 +393,12 @@
                     both_low[...] = (both - upper.astype(f32)).astype(bf16)
                 tail_out[sweep].wait_recv()
                 entering = split(recv_row[base_row + ITERS + sweep])
-                pass_on(tail_rows + times_pair(entering, both_high[...], both_low[...]))
+
+                @pl.when(not_bottom)
+                def _():
+                    onward = tail_rows + times_pair(entering, both_high[...], both_low[...])
+                    pass_on(onward + add_late())
+
                 above_row[...] = lead_rows + times_pair(entering, map_high[...], map_low[...])
 
         @pl.when(lead_before)
@@ -397,6 +410,8 @@
         def _():
             above_row[...] = jnp.zeros((SUB, cols), f32)
 
+        if sweep > 0:
+            base[-1] = base[-1] + late_change[...]
         above = above_row[...]
         entering = split(above * w_above)
         solved = [base[0] + times_transposed(entering, mats[0, :, :cols])]
@@ -450,7 +465,7 @@
     dma = pltpu.SemaphoreType.DMA
     return pl.pallas_call(
         functools.partial(kernel, n_strip, n_col),
-        out_shape=jax.ShapeDtypeStruct(positions.shape, f32),
+        out_shape=pltpu.VMEM(positions.shape, f32),
         in_specs=[pl.BlockSpec(memory_space=pltpu.HBM)] * 6,
         out_specs=pl.BlockSpec(memory_space=pltpu.VMEM),
         scratch_shapes=[
@@ -476,6 +491,7 @@
             pltpu.VMEM((cols, cols), bf16),
             pltpu.VMEM((cols, cols), bf16),
             pltpu.VMEM((SUB, cols), f32),
+            pltpu.VMEM((SUB, block), f32),
             dma((5,)),
             dma((strips,)),
             dma((ITERS, 2)),

time: 26.1 us -> 24.8 us (0.950)
  local copies, waits for them, and re-layouts: 1.35 us -> 0.61 us
  Pallas kernels: 24.5 us -> 23.8 us
    unnamed x1, local copies, waits for them, and re-layouts: 1.35 us -> 0.61 us
    pallas_call x1, Pallas kernels: 24.5 us -> 23.8 us  [shards(): pl.pallas_call(functools.partial(kernel, n_strip, n_col), out_shape=pltpu...]
where the time goes in v4:
time: 24.8 us; the launch traced here: 24.4 us
  Pallas kernels  23.8 us (96%)
  local copies, waits for them, and re-layouts  0.61 us (2%)
    pallas_call x1, Pallas kernels, shards(): pl.pallas_call(functools.partial(kernel, n_strip, n_col), out_shape=pltpu...  23.8 us
    unnamed x1, local copies, waits for them, and re-layouts  0.61 us

profile of v4, /device:TPU:24, one launch (start us, length us, event | category | flops | bytes accessed | tf_op | source)
XLA Modules:
  0.0 24.4 jit_solution(17617899212319595423)
XLA Ops:
  0.0 23.8 %shard_map.64 = f32[3,8,256]{2,1,0:T(8,128)S(1)} custom-call(s32[64]{0:T(128)} %pins_in.1, f32[3,8,256]{2,1,0:T(8,128)} %pos_in.1, f32[3,8,256]{2,1,0:T(8,128)} %tgt_in.1, f32[8,256]{1,0:T(8,128)} %inertia_in.1, f32[3,8,256]{2,1,0:T(8,128)} %stf_in.1, bf16[4,512,512]{2,1,0:T(8,128)(2,1)} %inv.1), custom_call_target="tpu_custom_call" | custom-call | tf_op jit(solution)/shard_map/pallas_call | solution.py:466
  23.8 0.6 %copy.8 = f32[3,8,256]{2,1,0:T(8,128)} copy(f32[3,8,256]{2,1,0:T(8,128)S(1)} %shard_map.64) | data formatting | bytes 49152

commit v5 on v4

--- a/solution.py
+++ b/solution.py
@@ -192,7 +192,7 @@
             high[k] = upper
             low[k] = (product - upper.astype(f32)).astype(bf16)
 
-    extend_product(0, strips // 2)
+    extend_product(0, strips - 1)
 
     neighbours = sum(there.astype(jnp.int32) for there, _ in sides)
     pl.semaphore_wait(barrier, neighbours)
@@ -214,7 +214,7 @@
     def _():
         ups[0].start()
 
-    extend_product(strips // 2, strips)
+    extend_product(strips - 1, strips)
 
     for fetch in fetches[2:]:
         fetch.wait()
@@ -360,8 +360,8 @@
         def pass_on(tail_rows):
             send_row[base_row + ITERS + sweep] = tail_rows * w_bottom
             send_row[base_row + 2 * ITERS + sweep] = tail_rows
+            send(next_out[sweep], is_tail & not_bottom)
             send(tail_out[sweep], tail_after)
-            send(next_out[sweep], is_tail & not_bottom)
 
         @pl.when(is_tail)
         def _():

time: 24.8 us -> 25.1 us (1.012)
  Pallas kernels: 23.8 us -> 24.1 us
    pallas_call x1, Pallas kernels: 23.8 us -> 24.1 us  [shards(): pl.pallas_call(functools.partial(kernel, n_strip, n_col), out_shape=pltpu...]
where the time goes in v5:
time: 25.1 us; the launch traced here: 24.7 us
  Pallas kernels  24.1 us (96%)
  local copies, waits for them, and re-layouts  0.61 us (2%)
    pallas_call x1, Pallas kernels, shards(): pl.pallas_call(functools.partial(kernel, n_strip, n_col), out_shape=pltpu...  24.1 us
    unnamed x1, local copies, waits for them, and re-layouts  0.61 us

profile of v5, /device:TPU:24, one launch (start us, length us, event | category | flops | bytes accessed | tf_op | source)
XLA Modules:
  0.0 24.7 jit_solution(13376878326729123466)
XLA Ops:
  0.0 24.1 %shard_map.64 = f32[3,8,256]{2,1,0:T(8,128)S(1)} custom-call(s32[64]{0:T(128)} %pins_in.1, f32[3,8,256]{2,1,0:T(8,128)} %pos_in.1, f32[3,8,256]{2,1,0:T(8,128)} %tgt_in.1, f32[8,256]{1,0:T(8,128)} %inertia_in.1, f32[3,8,256]{2,1,0:T(8,128)} %stf_in.1, bf16[4,512,512]{2,1,0:T(8,128)(2,1)} %inv.1), custom_call_target="tpu_custom_call" | custom-call | tf_op jit(solution)/shard_map/pallas_call | solution.py:466
  24.1 0.6 %copy.8 = f32[3,8,256]{2,1,0:T(8,128)} copy(f32[3,8,256]{2,1,0:T(8,128)S(1)} %shard_map.64) | data formatting | bytes 49152
